TPU v7x, 32 devices: a whole 2x2x4 slice. The times are simulated.
32 devices in a mesh: gx: 2 (over x), gy: 4 (over y, core), gz: 4 (over z).
Axes of the slice: x: 2, y: 2, z: 4, core: 2. Of those that a mesh axis runs over, the one named last changes fastest.
Arguments:
- right_side: float32 [4, 5, 2, 32, 512], P(None, None, 'gx', 'gy', 'gz'), may hold values from -6 to 6
- jacobian: bfloat16 [27, 5, 5, 2, 32, 512], P(None, None, None, 'gx', 'gy', 'gz'), may hold values from -0.14 to 12.14, as said below
Outputs:
- solution: float32 [4, 5, 2, 32, 512], P(None, None, 'gx', 'gy', 'gz')
- residual: float32 [4, 5, 2, 32, 512], P(None, None, 'gx', 'gy', 'gz')
Inputs may be any that keep to these rules, and one draw needn't show every extreme that they name: `jacobian`: blocks of offsets other than 13 and the off-diagonal entries of block 13 lie within -0.14 to 0.14; the diagonal entries of block 13 exceed 5.8 in every cell.
All inputs are finite; a program needn't handle non-finite values.
Results may differ from a plain program's by a relative error of at most 0.0003.
Values sent between devices are 32-bit elements.
A program may use at most 64 MiB of HBM per device.

v0:
```python
import functools
import itertools

import jax
import jax.numpy as jnp
from jax import lax
from jax.experimental import pallas as pl
from jax.experimental.pallas import tpu as pltpu
from jax.sharding import PartitionSpec as P

ITERS = 3
SHIFT = 9.0
MESH = pl.DeviceIdType.MESH
AXES = ("gx", "gy", "gz")


def make_kernel(sizes, rhs, comp, rows, lanes):
    count_x, count_y, count_z = sizes
    devices = count_x * count_y * count_z
    fields = rhs * comp
    merged = count_x == 2
    plane_steps = (0, 1) if merged else (0, 1, -1)
    planes = len(plane_steps)
    slots = 9 + rhs
    pair_list = []
    vectors = rhs * (ITERS + 1)
    for step in range(1, ITERS + 1):
        for mine in range(rhs * step, rhs * (step + 1)):
            for other in range(0, mine + 1):
                pair_list.append((mine, other))
    pair_slot = {pair: slot for slot, pair in enumerate(pair_list)}
    pair_pad = -(-len(pair_list) // 128) * 128

    def kernel(
        right_ref, jac_hbm, sol_ref, res_ref,
        basis, prods, jac_low, jac, shifted, packs, edge_rows, edge_corner,
        far_plane, halo_rows, halo_cols, halo_corner, tops, gram, part, parts,
        jac_sem, send_sem, recv_sem, red_send, red_recv,
    ):
        my_x, my_y, my_z = (lax.axis_index(axis) for axis in AXES)
        me = (my_x * count_y + my_y) * count_z + my_z

        def coords(index):
            return (index // (count_y * count_z), index // count_z % count_y, index % count_z)

        loads = pltpu.make_async_copy(jac_hbm, jac_low, jac_sem)
        loads.start()

        barrier = pltpu.get_barrier_semaphore()

        def greet(step, carry):
            pl.semaphore_signal(
                barrier, inc=1, device_id=coords(lax.rem(me + step, devices)), device_id_type=MESH
            )
            return carry

        lax.fori_loop(1, devices, greet, 0)

        lane = lax.broadcasted_iota(jnp.int32, (rows, lanes), 1)
        sub = lax.broadcasted_iota(jnp.int32, (rows, lanes), 0)

        def field(turn, at):
            return right_ref[at] if turn == 0 else basis[turn - 1, at]

        def pack(turn):
            packed = jnp.zeros((rows, lanes), jnp.float32)
            for at in range(fields):
                value = field(turn, at)
                edge_rows[turn, 0, at : at + 1, :] = value[rows - 1 : rows]
                edge_rows[turn, 1, at : at + 1, :] = value[0:1]
                packed = jnp.where(lane // 2 == at, pltpu.roll(value, 2 * at + 1, 1), packed)
            packs[turn] = packed
            edge_corner[turn, 0] = packed[rows - 1 : rows]
            edge_corner[turn, 1] = packed[0:1]

        def messages(turn):
            found = []
            for plane, step_x in enumerate(plane_steps):
                for dy, dz in itertools.product((1, -1, 0), (1, -1, 0)):
                    side_y = 0 if dy == 1 else 1
                    side_z = 0 if dz == 1 else 1
                    if dy == 0 and dz == 0:
                        if plane == 0:
                            continue
                        values = right_ref if turn == 0 else basis.at[turn - 1]
                        moves = [
                            (values.at[pl.ds(r * comp, comp)], far_plane.at[turn, plane - 1, pl.ds(r * comp, comp)])
                            for r in range(rhs)
                        ]
                    elif dz == 0:
                        moves = [(edge_rows.at[turn, side_y], halo_rows.at[turn, plane, side_y])]
                    elif dy == 0:
                        moves = [(packs.at[turn], halo_cols.at[turn, plane, side_z])]
                    else:
                        moves = [(edge_corner.at[turn, side_y], halo_corner.at[turn, plane, side_y, side_z])]
                    for part_at, (source, target) in enumerate(moves):
                        slot = plane * slots
                        if len(moves) == 1:
                            slot = slot + (dy + 1) * 3 + dz + 1
                        else:
                            slot = slot + 9 + part_at
                        copy = pltpu.make_async_remote_copy(
                            src_ref=source,
                            dst_ref=target,
                            send_sem=send_sem.at[turn, slot],
                            recv_sem=recv_sem.at[turn, slot],
                            device_id=(
                                lax.rem(my_x + step_x + count_x, count_x),
                                lax.rem(my_y + dy + count_y, count_y),
                                jnp.clip(my_z + dz, 0, count_z - 1),
                            ),
                            device_id_type=MESH,
                        )
                        found.append((plane, dz, copy, part_at if len(moves) > 1 else None))
            return found

        above = my_z < count_z - 1
        below = my_z > 0

        def for_each(copies, act, sending):
            for step_z in (1, -1, 0):
                chosen = [copy for _, dz, copy, _ in copies if dz == step_z]
                if step_z == 0:
                    for copy in chosen:
                        act(copy)
                else:
                    present = above if (step_z == 1) == sending else below

                    @pl.when(present)
                    def _():
                        for copy in chosen:
                            act(copy)

        def shift_edges(turn, plane):
            low = jnp.where(below, pltpu.roll(halo_cols[turn, plane, 0], 1, 1), 0.0)
            high = jnp.where(above, pltpu.roll(halo_cols[turn, plane, 1], lanes - 1, 1), 0.0)
            mixed = jnp.where(lane % 2 == 1, low, high)
            wide_lane = lax.broadcasted_iota(jnp.int32, (fields, lanes), 1)
            wide_at = lax.broadcasted_iota(jnp.int32, (fields, lanes), 0)
            for side in range(2):
                strip = halo_rows[turn, plane, side]
                low_row = jnp.where(below, halo_corner[turn, plane, side, 0], 0.0)
                high_row = jnp.where(above, halo_corner[turn, plane, side, 1], 0.0)
                low_col = jnp.sum(
                    jnp.where(wide_lane == 2 * wide_at, low_row, 0.0), axis=1, keepdims=True
                )
                high_col = jnp.sum(
                    jnp.where(wide_lane == 2 * wide_at + 1, high_row, 0.0), axis=1, keepdims=True
                )
                tops[side, 0] = jnp.where(wide_lane == 0, low_col, pltpu.roll(strip, 1, 1))
                tops[side, 1] = strip
                tops[side, 2] = jnp.where(
                    wide_lane == lanes - 1, high_col, pltpu.roll(strip, lanes - 1, 1)
                )
            return mixed

        def shift_fields(turn, plane, mixed, first, last):
            for at in range(first, last):
                value = field(turn, at) if plane == 0 else far_plane[turn, plane - 1, at]
                edge = pltpu.roll(mixed, lanes - 2 * at - 1, 1)
                along = (
                    jnp.where(lane == 0, edge, pltpu.roll(value, 1, 1)),
                    value,
                    jnp.where(lane == lanes - 1, edge, pltpu.roll(value, lanes - 1, 1)),
                )
                for dz in range(3):
                    shifted[dz, at] = jnp.where(
                        sub == 0, tops[0, dz, at : at + 1, :], pltpu.roll(along[dz], 1, 0)
                    )
                    shifted[3 + dz, at] = along[dz]
                    shifted[6 + dz, at] = jnp.where(
                        sub == rows - 1,
                        tops[1, dz, at : at + 1, :],
                        pltpu.roll(along[dz], rows - 1, 0),
                    )

        def stencil(plane, totals, sides):
            def body(line, sums):
                sums = list(sums)
                for near, source in itertools.product(range(3), range(comp)):
                    near = line * 3 + near
                    blocks = [jac[plane, near, a * comp + source] for a in range(comp)]
                    for place, r in enumerate(sides):
                        value = shifted[near, r * comp + source]
                        for a in range(comp):
                            sums[place * comp + a] = sums[place * comp + a] + blocks[a] * value
                return tuple(sums)

            return list(lax.fori_loop(0, 3, body, tuple(totals)))

        def vector(index, c):
            if index < rhs:
                return right_ref[index * comp + c]
            return prods[index // rhs - 1, (index % rhs) * comp + c]

        def dots(step):
            for mine in range(rhs * step, rhs * (step + 1)):
                own = [vector(mine, c) for c in range(comp)]
                for other in range(0, mine + 1):
                    total = own[0] * vector(other, 0)
                    for c in range(1, comp):
                        total = total + own[c] * vector(other, c)
                    gram[pair_slot[mine, other]] = total

        for slot in range(len(pair_list), pair_pad):
            gram[slot] = jnp.zeros((rows, lanes), jnp.float32)
        pack(0)
        loads.wait()

        def widen(near, carry):
            for entry in range(comp * comp):
                jac[0, near, entry] = jac_low[9 + near, entry].astype(jnp.float32)
                first = jac_low[near, entry].astype(jnp.float32)
                last = jac_low[18 + near, entry].astype(jnp.float32)
                if merged:
                    jac[1, near, entry] = first + last
                else:
                    jac[1, near, entry] = first
                    jac[2, near, entry] = last
            return carry

        lax.fori_loop(0, 9, widen, 0)
        pl.semaphore_wait(barrier, devices - 1)

        for turn in range(ITERS):
            copies = messages(turn)
            for_each(copies, lambda copy: copy.start(), True)
            if turn > 0:
                dots(turn)
            totals = [jnp.zeros((rows, lanes), jnp.float32) for _ in range(fields)]
            for plane in range(planes):
                mine = [copy for copy in copies if copy[0] == plane and copy[3] is None]
                for_each(mine, lambda copy: copy.wait_recv(), False)
                mixed = shift_edges(turn, plane)
                if plane == 0:
                    shift_fields(turn, plane, mixed, 0, fields)
                    totals = stencil(plane, totals, range(rhs))
                    for at in range(fields):
                        prods[turn, at] = totals[at]
                    continue
                for r in range(rhs):
                    for copy in copies:
                        if copy[0] == plane and copy[3] == r:
                            copy[2].wait_recv()
                    span = range(r * comp, (r + 1) * comp)
                    shift_fields(turn, plane, mixed, span.start, span.stop)
                    sums = stencil(plane, [prods[turn, at] for at in span], (r,))
                    for at, value in zip(span, sums):
                        prods[turn, at] = value
                        if turn < ITERS - 1 and plane == planes - 1:
                            basis[turn, at] = value - SHIFT * field(turn, at)
            if turn < ITERS - 1:
                pack(turn + 1)

        dots(ITERS)
        sums = jnp.sum(gram[...], axis=1)
        row = lax.dot_general(
            jnp.ones((rows, lanes), jnp.float32),
            sums,
            (((1,), (1,)), ((), ())),
            precision=lax.Precision.HIGHEST,
            preferred_element_type=jnp.float32,
        )
        part[...] = row[0:1]

        def spread(step):
            return pltpu.make_async_remote_copy(
                src_ref=part,
                dst_ref=parts.at[me],
                send_sem=red_send.at[step],
                recv_sem=red_recv.at[step],
                device_id=coords(lax.rem(me + step, devices)),
                device_id_type=MESH,
            )

        def gathered(step):
            return pltpu.make_async_remote_copy(
                src_ref=part,
                dst_ref=parts.at[lax.rem(me + devices - step, devices)],
                send_sem=red_send.at[step],
                recv_sem=red_recv.at[step],
                device_id=coords(lax.rem(me + step, devices)),
                device_id_type=MESH,
            )

        def begin(step, carry):
            spread(step).start()
            return carry

        def finish(step, carry):
            gathered(step).wait_recv()
            return carry

        lax.fori_loop(1, devices, begin, 0)
        parts[me] = part[...]
        lax.fori_loop(1, devices, finish, 0)
        total_row = jnp.broadcast_to(jnp.sum(parts[...], axis=0), (rows, pair_pad))

        def entry(mine, other):
            slot = pair_slot[max(mine, other), min(mine, other)]
            return jnp.broadcast_to(total_row[:, slot : slot + 1], (rows, lanes))

        size = rhs * ITERS
        matrix = {}
        target = {}
        for i in range(size):
            for j in range(i + 1):
                matrix[i, j] = entry(rhs + i, rhs + j)
            for r in range(rhs):
                target[i, r] = entry(rhs + i, r)
        inverse = {}
        for k in range(size):
            inverse[k] = 1.0 / matrix[k, k]
            for i in range(k + 1, size):
                ratio = matrix[i, k] * inverse[k]
                for j in range(k + 1, i + 1):
                    matrix[i, j] = matrix[i, j] - ratio * matrix[j, k]
                for r in range(rhs):
                    target[i, r] = target[i, r] - ratio * target[k, r]
        weights = {}
        for k in range(size - 1, -1, -1):
            for r in range(rhs):
                accum = target[k, r]
                for later in range(k + 1, size):
                    accum = accum - matrix[later, k] * weights[later, r]
                weights[k, r] = accum * inverse[k]
        for r in range(rhs):
            for c in range(comp):
                found = jnp.zeros((rows, lanes), jnp.float32)
                left = right_ref[r * comp + c]
                for j in range(size):
                    found = found + weights[j, r] * field(j // rhs, (j % rhs) * comp + c)
                    left = left - weights[j, r] * prods[j // rhs, (j % rhs) * comp + c]
                sol_ref[r * comp + c] = found
                res_ref[r * comp + c] = left

        for turn in range(ITERS):
            for_each(messages(turn), lambda copy: copy.wait_send(), True)

        def settle(step, carry):
            spread(step).wait_send()
            return carry

        lax.fori_loop(1, devices, settle, 0)

    full = (rows, lanes)
    scratch = [
        pltpu.VMEM((ITERS - 1, fields) + full, jnp.float32),
        pltpu.VMEM((ITERS, fields) + full, jnp.float32),
        pltpu.VMEM((27, comp * comp) + full, jnp.bfloat16),
        pltpu.VMEM((planes, 9, comp * comp) + full, jnp.float32),
        pltpu.VMEM((9, fields) + full, jnp.float32),
        pltpu.VMEM((ITERS,) + full, jnp.float32),
        pltpu.VMEM((ITERS, 2, fields, lanes), jnp.float32),
        pltpu.VMEM((ITERS, 2, 1, lanes), jnp.float32),
        pltpu.VMEM((ITERS, planes - 1, fields) + full, jnp.float32),
        pltpu.VMEM((ITERS, planes, 2, fields, lanes), jnp.float32),
        pltpu.VMEM((ITERS, planes, 2) + full, jnp.float32),
        pltpu.VMEM((ITERS, planes, 2, 2, 1, lanes), jnp.float32),
        pltpu.VMEM((2, 3, fields, lanes), jnp.float32),
        pltpu.VMEM((pair_pad,) + full, jnp.float32),
        pltpu.VMEM((1, pair_pad), jnp.float32),
        pltpu.VMEM((devices, 1, pair_pad), jnp.float32),
        pltpu.SemaphoreType.DMA,
        pltpu.SemaphoreType.DMA((ITERS, planes * slots)),
        pltpu.SemaphoreType.DMA((ITERS, planes * slots)),
        pltpu.SemaphoreType.DMA((devices,)),
        pltpu.SemaphoreType.DMA((devices,)),
    ]
    return kernel, scratch


def hand_over(found_ref, left_ref, sol_ref, res_ref):
    sol_ref[...] = found_ref[...]
    res_ref[...] = left_ref[...]


def shards(sizes, right_side, jacobian):
    rhs, comp, extent_x, rows, lanes = right_side.shape
    assert extent_x == 1
    kernel, scratch = make_kernel(sizes, rhs, comp, rows, lanes)
    shape = jax.ShapeDtypeStruct((rhs * comp, rows, lanes), jnp.float32)
    vmem = pl.BlockSpec(memory_space=pltpu.VMEM)
    found, left = pl.pallas_call(
        kernel,
        out_shape=(shape, shape),
        in_specs=[vmem, pl.BlockSpec(memory_space=pl.ANY)],
        out_specs=(vmem, vmem),
        scratch_shapes=scratch,
        compiler_params=pltpu.CompilerParams(collective_id=0, has_side_effects=True),
    )(
        right_side.reshape(rhs * comp, rows, lanes),
        jacobian.reshape(27, comp * comp, rows, lanes),
    )
    found, left = pl.pallas_call(
        hand_over,
        out_shape=(shape, shape),
        in_specs=[vmem, vmem],
        out_specs=(vmem, vmem),
    )(found, left)
    return found.reshape(right_side.shape), left.reshape(right_side.shape)


def solution(mesh):
    sizes = tuple(mesh.shape[axis] for axis in AXES)
    in_specs = (P(None, None, *AXES), P(None, None, None, *AXES))
    out_specs = (P(None, None, *AXES), P(None, None, *AXES))
    return jax.shard_map(
        functools.partial(shards, sizes), mesh=mesh, in_specs=in_specs, out_specs=out_specs, check_vma=False
    )
```

profile of v0, /device:TPU:0, one launch (start us, length us, event | category | flops | bytes accessed | tf_op | source)
XLA Modules:
  0.0 31.1 jit_solution(2583391599497552359)
XLA Ops:
  0.6 28.9 %shard_map.41 = (f32[20,8,128]{2,1,0:T(8,128)}, f32[20,8,128]{2,1,0:T(8,128)}) custom-call(f32[20,8,128]{2,1,0:T(8,128)} %bitcast.9, bf16[27,25,8,128]{3,2,1,0:T(8,128)(2,1)} %bitcast.8), custom_call_target="tpu_custom_call" | custom-call | tf_op jit(solution)/shard_map/pallas_call | solution.py:384
  29.5 1.6 %shard_map.42 = (f32[20,8,128]{2,1,0:T(8,128)}, f32[20,8,128]{2,1,0:T(8,128)}) custom-call(f32[20,8,128]{2,1,0:T(8,128)} %get-tuple-element.6.found_ref, f32[20,8,128]{2,1,0:T(8,128)} %get-tuple-element.7.left_ref), custom_call_target="tpu_custom_call" | custom-call | tf_op jit(solution)/shard_map/pallas_call | solution.py:395
where the time goes:
time: 31.3 us; the launch traced here: 31.1 us
  Pallas kernels  30.5 us (97%)
  between operations  0.64 us (2%)
    pallas_call x1, Pallas kernels, shards(): pl.pallas_call(kernel, out_shape=(shape, shape), in_specs=[vmem, pl.Block...  28.9 us
    pallas_call x1, Pallas kernels, shards(): pl.pallas_call(hand_over, out_shape=(shape, shape), in_specs=[vmem, vmem]...  1.6 us

commit v1 on v0

--- a/solution.py
+++ b/solution.py
@@ -19,6 +19,7 @@
     devices = count_x * count_y * count_z
     fields = rhs * comp
     merged = count_x == 2
+    near_only = max(count_x // 2, count_y // 2, count_z - 1) <= ITERS
     plane_steps = (0, 1) if merged else (0, 1, -1)
     planes = len(plane_steps)
     slots = 9 + rhs
@@ -32,10 +33,10 @@
     pair_pad = -(-len(pair_list) // 128) * 128
 
     def kernel(
-        right_ref, jac_hbm, sol_ref, res_ref,
-        basis, prods, jac_low, jac, shifted, packs, edge_rows, edge_corner,
+        right_hbm, jac_hbm, sol_ref, res_ref,
+        right_ref, basis, prods, jac_low, jac, shifted, packs, edge_rows, edge_corner,
         far_plane, halo_rows, halo_cols, halo_corner, tops, gram, part, parts,
-        jac_sem, send_sem, recv_sem, red_send, red_recv,
+        right_sem, jac_sem, send_sem, recv_sem, red_send, red_recv,
     ):
         my_x, my_y, my_z = (lax.axis_index(axis) for axis in AXES)
         me = (my_x * count_y + my_y) * count_z + my_z
@@ -43,18 +44,50 @@
         def coords(index):
             return (index // (count_y * count_z), index // count_z % count_y, index % count_z)
 
+        def beside(step_x, dy, dz):
+            return (
+                lax.rem(my_x + step_x + count_x, count_x),
+                lax.rem(my_y + dy + count_y, count_y),
+                jnp.clip(my_z + dz, 0, count_z - 1),
+            )
+
+        above = my_z < count_z - 1
+        below = my_z > 0
+        barrier = pltpu.get_barrier_semaphore()
+
+        def salute(device):
+            pl.semaphore_signal(barrier, inc=1, device_id=device, device_id_type=MESH)
+
+        if near_only:
+            for dz in (1, -1, 0):
+                offsets = [
+                    (step_x, dy)
+                    for step_x, dy in itertools.product(reversed(plane_steps), (1, -1, 0))
+                    if (step_x, dy, dz) != (0, 0, 0)
+                ]
+
+                def greet_layer():
+                    for step_x, dy in offsets:
+                        salute(beside(step_x, dy, dz))
+
+                if dz == 0:
+                    greet_layer()
+                else:
+                    pl.when(above if dz == 1 else below)(greet_layer)
+            greeted = planes * 3 * (1 + above.astype(jnp.int32) + below.astype(jnp.int32)) - 1
+        else:
+
+            def greet(step, carry):
+                salute(coords(lax.rem(me + step, devices)))
+                return carry
+
+            lax.fori_loop(1, devices, greet, 0)
+            greeted = devices - 1
+
+        right_load = pltpu.make_async_copy(right_hbm, right_ref, right_sem)
+        right_load.start()
         loads = pltpu.make_async_copy(jac_hbm, jac_low, jac_sem)
         loads.start()
-
-        barrier = pltpu.get_barrier_semaphore()
-
-        def greet(step, carry):
-            pl.semaphore_signal(
-                barrier, inc=1, device_id=coords(lax.rem(me + step, devices)), device_id_type=MESH
-            )
-            return carry
-
-        lax.fori_loop(1, devices, greet, 0)
 
         lane = lax.broadcasted_iota(jnp.int32, (rows, lanes), 1)
         sub = lax.broadcasted_iota(jnp.int32, (rows, lanes), 0)
@@ -104,18 +137,11 @@
                             dst_ref=target,
                             send_sem=send_sem.at[turn, slot],
                             recv_sem=recv_sem.at[turn, slot],
-                            device_id=(
-                                lax.rem(my_x + step_x + count_x, count_x),
-                                lax.rem(my_y + dy + count_y, count_y),
-                                jnp.clip(my_z + dz, 0, count_z - 1),
-                            ),
+                            device_id=beside(step_x, dy, dz),
                             device_id_type=MESH,
                         )
                         found.append((plane, dz, copy, part_at if len(moves) > 1 else None))
             return found
-
-        above = my_z < count_z - 1
-        below = my_z > 0
 
         def for_each(copies, act, sending):
             for step_z in (1, -1, 0):
@@ -204,7 +230,10 @@
 
         for slot in range(len(pair_list), pair_pad):
             gram[slot] = jnp.zeros((rows, lanes), jnp.float32)
+        right_load.wait()
         pack(0)
+        pl.semaphore_wait(barrier, greeted)
+        for_each(messages(0), lambda copy: copy.start(), True)
         loads.wait()
 
         def widen(near, carry):
@@ -220,12 +249,11 @@
             return carry
 
         lax.fori_loop(0, 9, widen, 0)
-        pl.semaphore_wait(barrier, devices - 1)
 
         for turn in range(ITERS):
             copies = messages(turn)
-            for_each(copies, lambda copy: copy.start(), True)
             if turn > 0:
+                for_each(copies, lambda copy: copy.start(), True)
                 dots(turn)
             totals = [jnp.zeros((rows, lanes), jnp.float32) for _ in range(fields)]
             for plane in range(planes):
@@ -263,38 +291,59 @@
         )
         part[...] = row[0:1]
 
-        def spread(step):
+        def reduce_copy(step, towards, source):
             return pltpu.make_async_remote_copy(
                 src_ref=part,
-                dst_ref=parts.at[me],
+                dst_ref=parts.at[source],
                 send_sem=red_send.at[step],
                 recv_sem=red_recv.at[step],
-                device_id=coords(lax.rem(me + step, devices)),
+                device_id=towards,
                 device_id_type=MESH,
             )
 
-        def gathered(step):
-            return pltpu.make_async_remote_copy(
-                src_ref=part,
-                dst_ref=parts.at[lax.rem(me + devices - step, devices)],
-                send_sem=red_send.at[step],
-                recv_sem=red_recv.at[step],
-                device_id=coords(lax.rem(me + step, devices)),
-                device_id_type=MESH,
+        if devices <= 64:
+            offsets = sorted(
+                itertools.product(range(count_x), range(count_y), range(count_z)),
+                key=lambda at: (-min(at[1], count_y - at[1]), -at[0], at[2]),
             )
-
-        def begin(step, carry):
-            spread(step).start()
-            return carry
-
-        def finish(step, carry):
-            gathered(step).wait_recv()
-            return carry
-
-        lax.fori_loop(1, devices, begin, 0)
+            peers = []
+            for step, (ox, oy, oz) in enumerate(offsets):
+                if (ox, oy, oz) == (0, 0, 0):
+                    continue
+                towards = (
+                    lax.rem(my_x + ox, count_x), lax.rem(my_y + oy, count_y), lax.rem(my_z + oz, count_z)
+                )
+                from_x = lax.rem(my_x + count_x - ox, count_x)
+                from_y = lax.rem(my_y + count_y - oy, count_y)
+                from_z = lax.rem(my_z + count_z - oz, count_z)
+                peers.append((step, towards, (from_x * count_y + from_y) * count_z + from_z))
+
+            def for_peers(act, sending):
+                for step, towards, source in peers:
+                    act(reduce_copy(step, towards, me if sending else source))
+        else:
+
+            def for_peers(act, sending):
+                def one(step, carry):
+                    source = me if sending else lax.rem(me + devices - step, devices)
+                    act(reduce_copy(step, coords(lax.rem(me + step, devices)), source))
+                    return carry
+
+                lax.fori_loop(1, devices, one, 0)
+
+        for_peers(lambda copy: copy.start(), True)
         parts[me] = part[...]
-        lax.fori_loop(1, devices, finish, 0)
-        total_row = jnp.broadcast_to(jnp.sum(parts[...], axis=0), (rows, pair_pad))
+        for_peers(lambda copy: copy.wait_recv(), False)
+        found_parts = parts[...]
+        count = devices
+        while count > 1:
+            half = count // 2
+            rest = found_parts[2 * half :]
+            found_parts = found_parts[:half] + found_parts[half : 2 * half]
+            if count % 2:
+                found_parts = jnp.concatenate([found_parts, rest], axis=0)
+            count = count - half
+        total_row = jnp.broadcast_to(found_parts[0], (rows, pair_pad))
 
         def entry(mine, other):
             slot = pair_slot[max(mine, other), min(mine, other)]
@@ -337,14 +386,11 @@
         for turn in range(ITERS):
             for_each(messages(turn), lambda copy: copy.wait_send(), True)
 
-        def settle(step, carry):
-            spread(step).wait_send()
-            return carry
-
-        lax.fori_loop(1, devices, settle, 0)
+        for_peers(lambda copy: copy.wait_send(), True)
 
     full = (rows, lanes)
     scratch = [
+        pltpu.VMEM((fields,) + full, jnp.float32),
         pltpu.VMEM((ITERS - 1, fields) + full, jnp.float32),
         pltpu.VMEM((ITERS, fields) + full, jnp.float32),
         pltpu.VMEM((27, comp * comp) + full, jnp.bfloat16),
@@ -362,6 +408,7 @@
         pltpu.VMEM((1, pair_pad), jnp.float32),
         pltpu.VMEM((devices, 1, pair_pad), jnp.float32),
         pltpu.SemaphoreType.DMA,
+        pltpu.SemaphoreType.DMA,
         pltpu.SemaphoreType.DMA((ITERS, planes * slots)),
         pltpu.SemaphoreType.DMA((ITERS, planes * slots)),
         pltpu.SemaphoreType.DMA((devices,)),
@@ -370,33 +417,42 @@
     return kernel, scratch
 
 
-def hand_over(found_ref, left_ref, sol_ref, res_ref):
-    sol_ref[...] = found_ref[...]
-    res_ref[...] = left_ref[...]
+def hand_over(found_ref, left_ref, sol_ref, res_ref, sem):
+    copies = [
+        pltpu.make_async_copy(found_ref, sol_ref, sem.at[0]),
+        pltpu.make_async_copy(left_ref, res_ref, sem.at[1]),
+    ]
+    for copy in copies:
+        copy.start()
+    for copy in copies:
+        copy.wait()
 
 
 def shards(sizes, right_side, jacobian):
     rhs, comp, extent_x, rows, lanes = right_side.shape
     assert extent_x == 1
     kernel, scratch = make_kernel(sizes, rhs, comp, rows, lanes)
-    shape = jax.ShapeDtypeStruct((rhs * comp, rows, lanes), jnp.float32)
+    shape = (rhs * comp, rows, lanes)
     vmem = pl.BlockSpec(memory_space=pltpu.VMEM)
+    hbm = pl.BlockSpec(memory_space=pltpu.HBM)
     found, left = pl.pallas_call(
         kernel,
-        out_shape=(shape, shape),
-        in_specs=[vmem, pl.BlockSpec(memory_space=pl.ANY)],
+        out_shape=(pltpu.VMEM(shape, jnp.float32),) * 2,
+        in_specs=[hbm, hbm],
         out_specs=(vmem, vmem),
         scratch_shapes=scratch,
         compiler_params=pltpu.CompilerParams(collective_id=0, has_side_effects=True),
     )(
-        right_side.reshape(rhs * comp, rows, lanes),
+        right_side.reshape(shape),
         jacobian.reshape(27, comp * comp, rows, lanes),
     )
     found, left = pl.pallas_call(
         hand_over,
-        out_shape=(shape, shape),
+        out_shape=(jax.ShapeDtypeStruct(shape, jnp.float32),) * 2,
         in_specs=[vmem, vmem],
-        out_specs=(vmem, vmem),
+        out_specs=(hbm, hbm),
+        scratch_shapes=[pltpu.SemaphoreType.DMA((2,))],
+        compiler_params=pltpu.CompilerParams(vmem_limit_bytes=24 * 2**20),
     )(found, left)
     return found.reshape(right_side.shape), left.reshape(right_side.shape)
 

time: 31.3 us -> 28.3 us (0.904)
  Pallas kernels: 30.5 us -> 27.5 us
    pallas_call x2, Pallas kernels: 30.5 us -> 27.5 us  [the longest x1 26.9 us: shards(): pl.pallas_call(kernel, out_shape=(pltpu.VMEM(shape, jnp.float32),) * 2, i...]
where the time goes in v1:
time: 28.3 us; the launch traced here: 28.2 us
  Pallas kernels  27.5 us (97%)
  between operations  0.64 us (2%)
    pallas_call x1, Pallas kernels, shards(): pl.pallas_call(kernel, out_shape=(pltpu.VMEM(shape, jnp.float32),) * 2, i...  26.9 us
    pallas_call x1, Pallas kernels, shards(): pl.pallas_call(hand_over, out_shape=(jax.ShapeDtypeStruct(shape, jnp.floa...  0.68 us

profile of v1, /device:TPU:0, one launch (start us, length us, event | category | flops | bytes accessed | tf_op | source)
XLA Modules:
  0.0 28.2 jit_solution(7360044761204612937)
XLA Ops:
  0.6 26.9 %shard_map.41 = (f32[20,8,128]{2,1,0:T(8,128)S(1)}, f32[20,8,128]{2,1,0:T(8,128)S(1)}) custom-call(f32[20,8,128]{2,1,0:T(8,128)} %bitcast.9, bf16[27,25,8,128]{3,2,1,0:T(8,128)(2,1)} %bitcast.8), custom_call_target="tpu_custom_call" | custom-call | tf_op jit(solution)/shard_map/pallas_call | solution.py:438
  27.5 0.7 %shard_map.42 = (f32[20,8,128]{2,1,0:T(8,128)}, f32[20,8,128]{2,1,0:T(8,128)}) custom-call(f32[20,8,128]{2,1,0:T(8,128)S(1)} %get-tuple-element.6.found_ref, f32[20,8,128]{2,1,0:T(8,128)S(1)} %get-tuple-element.7.left_ref), custom_call_target="tpu_custom_call" | custom-call | tf_op jit(solution)/shard_map/pallas_call | solution.py:449

commit v2 on v1

v2 whole, which is shorter than its diff:
```python
import functools
import itertools

import jax
import jax.numpy as jnp
from jax import lax
from jax.experimental import pallas as pl
from jax.experimental.pallas import tpu as pltpu
from jax.sharding import PartitionSpec as P

ITERS = 3
SHIFT = 9.0
MESH = pl.DeviceIdType.MESH
AXES = ("gx", "gy", "gz")
GROUPS = 4
KINDS = 6


def make_kernel(sizes, rhs, comp, rows, lanes):
    count_x, count_y, count_z = sizes
    devices = count_x * count_y * count_z
    fields = rhs * comp
    merged = count_x == 2
    near_only = max(count_x // 2, count_y // 2, count_z - 1) <= ITERS
    plane_steps = (0, 1) if merged else (0, 1, -1)
    planes = len(plane_steps)
    groups = GROUPS if rhs % GROUPS == 0 else rhs
    each = rhs // groups
    span = each * comp
    pair_list = []
    for mine in range(rhs, rhs * (ITERS + 1)):
        for other in range(0, mine + 1):
            pair_list.append((mine, other))
    pair_slot = {pair: slot for slot, pair in enumerate(pair_list)}
    pair_pad = -(-len(pair_list) // 128) * 128
    full = (rows, lanes)

    def kernel(
        right_hbm, jac_hbm, sol_ref, res_ref,
        right_ref, basis, prods, jac_low, jac, packs,
        far_plane, halo_rows, halo_cols, halo_corner, sums, part, parts,
        right_sem, jac_sem, send_sem, recv_sem, red_send, red_recv,
    ):
        my_x, my_y, my_z = (lax.axis_index(axis) for axis in AXES)
        me = (my_x * count_y + my_y) * count_z + my_z

        def coords(index):
            return (index // (count_y * count_z), index // count_z % count_y, index % count_z)

        def beside(step_x, dy, dz):
            return (
                lax.rem(my_x + step_x + count_x, count_x),
                lax.rem(my_y + dy + count_y, count_y),
                jnp.clip(my_z + dz, 0, count_z - 1),
            )

        above = my_z < count_z - 1
        below = my_z > 0

        def in_layer(dz, act):
            if dz == 0:
                act()
            else:
                pl.when(above if dz == 1 else below)(act)

        barrier = pltpu.get_barrier_semaphore()

        def salute(device):
            pl.semaphore_signal(barrier, inc=1, device_id=device, device_id_type=MESH)

        if near_only:
            for dz in (1, -1, 0):
                def greet_layer():
                    for step_x, dy in itertools.product(reversed(plane_steps), (1, -1, 0)):
                        if (step_x, dy, dz) != (0, 0, 0):
                            salute(beside(step_x, dy, dz))

                in_layer(dz, greet_layer)
            greeted = planes * 3 * (1 + above.astype(jnp.int32) + below.astype(jnp.int32)) - 1
        else:

            def greet(step, carry):
                salute(coords(lax.rem(me + step, devices)))
                return carry

            lax.fori_loop(1, devices, greet, 0)
            greeted = devices - 1

        right_load = pltpu.make_async_copy(right_hbm, right_ref, right_sem)
        right_load.start()
        loads = pltpu.make_async_copy(jac_hbm, jac_low, jac_sem)
        loads.start()

        lane = lax.broadcasted_iota(jnp.int32, full, 1)
        sub = lax.broadcasted_iota(jnp.int32, full, 0)

        def values(turn):
            return right_ref if turn == 0 else basis.at[turn - 1]

        def pack(turn, group, found):
            packed = jnp.zeros(full, jnp.float32)
            for at in range(span):
                packed = jnp.where(lane // 2 == at, pltpu.roll(found[at], 2 * at + 1, 1), packed)
            packs[turn, group] = packed

        def remote(source, target, kind, turn, group, device):
            return pltpu.make_async_remote_copy(
                src_ref=source,
                dst_ref=target,
                send_sem=send_sem.at[kind % KINDS],
                recv_sem=recv_sem.at[turn, group, kind],
                device_id=device,
                device_id_type=MESH,
            )

        def send(turn, group):
            mine = pl.ds(group * span, span)
            for dz in (1, -1, 0):
                side_z = 0 if dz == 1 else 1

                def layer():
                    for plane in reversed(range(planes)):
                        kind = KINDS * plane
                        for dy in (1, -1, 0):
                            device = beside(plane_steps[plane], dy, dz)
                            edge = pl.ds(rows - 1 if dy == 1 else 0, 1)
                            place = pl.ds(0 if dy == 1 else rows - 1, 1)
                            if dy == 0 and dz == 0:
                                continue
                            if dz == 0:
                                copy = remote(
                                    values(turn).at[mine, edge], halo_rows.at[turn, group, plane, :, place],
                                    kind, turn, group, device,
                                )
                            elif dy == 0:
                                copy = remote(
                                    packs.at[turn, group], halo_cols.at[turn, group, plane, side_z],
                                    kind + 1 + side_z, turn, group, device,
                                )
                            else:
                                copy = remote(
                                    packs.at[turn, group, edge], halo_corner.at[turn, group, plane, side_z, place],
                                    kind + 3 + side_z, turn, group, device,
                                )
                            copy.start()

                in_layer(dz, layer)
            for plane in range(1, planes):
                remote(
                    values(turn).at[mine], far_plane.at[turn, group, plane - 1],
                    KINDS * plane + 5, turn, group, beside(plane_steps[plane], 0, 0),
                ).start()

        def wait_edges(turn, group, plane):
            kind = KINDS * plane
            here = beside(1, 0, 0)
            both = halo_rows.at[turn, group, plane, :, pl.ds(0, 2)]
            remote(both, both, kind, turn, group, here).wait_recv()
            for side_z, dz in ((0, -1), (1, 1)):

                def layer():
                    column = halo_cols.at[turn, group, plane, side_z]
                    remote(column, column, kind + 1 + side_z, turn, group, here).wait_recv()
                    corner = halo_corner.at[turn, group, plane, side_z, pl.ds(0, 2)]
                    remote(corner, corner, kind + 3 + side_z, turn, group, here).wait_recv()

                in_layer(dz, layer)

        def wait_far(turn, group, plane):
            whole = far_plane.at[turn, group, plane - 1]
            remote(whole, whole, KINDS * plane + 5, turn, group, beside(1, 0, 0)).wait_recv()

        def turned(value, way):
            if way == 0:
                return value
            return pltpu.roll(value, 1 if way < 0 else rows - 1, 0)

        def stencil(turn, group, plane, totals):
            low = jnp.where(below, pltpu.roll(halo_cols[turn, group, plane, 0], 1, 1), 0.0)
            high = jnp.where(above, pltpu.roll(halo_cols[turn, group, plane, 1], lanes - 1, 1), 0.0)
            mixed = jnp.where(lane % 2 == 1, low, high)
            low = jnp.where(below, pltpu.roll(halo_corner[turn, group, plane, 0], 1, 1), 0.0)
            high = jnp.where(above, pltpu.roll(halo_corner[turn, group, plane, 1], lanes - 1, 1), 0.0)
            outer = jnp.where(lane % 2 == 1, low, high)
            side = {-1: sub == 0, 1: sub == rows - 1}
            columns = {0: mixed}
            for dy in (-1, 1):
                columns[dy] = jnp.where(side[dy], outer, turned(mixed, dy))
            for at in range(span):
                source = at % comp
                r = at // comp
                if plane == 0:
                    value = values(turn)[group * span + at]
                else:
                    value = far_plane[turn, group, plane - 1, at]
                beyond = halo_rows[turn, group, plane, at]
                for dy in (0, -1, 1):
                    line = value if dy == 0 else jnp.where(side[dy], beyond, turned(value, dy))
                    edge = pltpu.roll(columns[dy], lanes - 2 * at - 1, 1)
                    along = (
                        jnp.where(lane == 0, edge, pltpu.roll(line, 1, 1)),
                        line,
                        jnp.where(lane == lanes - 1, edge, pltpu.roll(line, lanes - 1, 1)),
                    )
                    for dz in range(3):
                        near = (dy + 1) * 3 + dz
                        for a in range(comp):
                            found = jac[plane, near, a * comp + source] * along[dz]
                            key = (r * comp + a, (source + dz) % 2)
                            totals[key] = totals[key] + found if key in totals else found
            return totals

        def vector(index, c):
            if index < rhs:
                return right_ref[index * comp + c]
            return prods[index // rhs - 1, (index % rhs) * comp + c]

        def dots(mine):
            own = [vector(mine, c) for c in range(comp)]
            for other in range(0, mine + 1):
                total = own[0] * vector(other, 0)
                for c in range(1, comp):
                    total = total + own[c] * vector(other, c)
                slot = pair_slot[mine, other]
                sums[slot : slot + 1, :] = jnp.sum(total, axis=0, keepdims=True)

        for slot in range(len(pair_list), pair_pad):
            sums[slot : slot + 1, :] = jnp.zeros((1, lanes), jnp.float32)
        right_load.wait()
        for group in range(groups):
            pack(0, group, [right_ref[group * span + at] for at in range(span)])
        pl.semaphore_wait(barrier, greeted)
        for group in range(groups):
            send(0, group)
        loads.wait()

        def widen(near, carry):
            for entry in range(comp * comp):
                jac[0, near, entry] = jac_low[9 + near, entry].astype(jnp.float32)
                first = jac_low[near, entry].astype(jnp.float32)
                last = jac_low[18 + near, entry].astype(jnp.float32)
                if merged:
                    jac[1, near, entry] = first + last
                else:
                    jac[1, near, entry] = first
                    jac[2, near, entry] = last
            return carry

        lax.fori_loop(0, 9, widen, 0)

        for turn in range(ITERS):
            for group in range(groups):
                totals = {}
                for plane in range(planes):
                    wait_edges(turn, group, plane)
                    if plane > 0:
                        wait_far(turn, group, plane)
                    totals = stencil(turn, group, plane, totals)
                found = [totals[at, 0] + totals[at, 1] for at in range(span)]
                for at in range(span):
                    prods[turn, group * span + at] = found[at]
                if turn < ITERS - 1:
                    found = [found[at] - SHIFT * values(turn)[group * span + at] for at in range(span)]
                    for at in range(span):
                        basis[turn, group * span + at] = found[at]
                    pack(turn + 1, group, found)
                    send(turn + 1, group)
                for r in range(group * each, (group + 1) * each):
                    dots(rhs * (turn + 1) + r)

        part[...] = jnp.sum(jnp.transpose(sums[...]), axis=0, keepdims=True)
        def reduce_copy(step, towards, source):
            return pltpu.make_async_remote_copy(
                src_ref=part,
                dst_ref=parts.at[source],
                send_sem=red_send.at[step],
                recv_sem=red_recv.at[step],
                device_id=towards,
                device_id_type=MESH,
            )

        if devices <= 64:
            offsets = sorted(
                itertools.product(range(count_x), range(count_y), range(count_z)),
                key=lambda at: (-min(at[1], count_y - at[1]), -at[0], at[2]),
            )
            peers = []
            for step, (ox, oy, oz) in enumerate(offsets):
                if (ox, oy, oz) == (0, 0, 0):
                    continue
                towards = (
                    lax.rem(my_x + ox, count_x), lax.rem(my_y + oy, count_y), lax.rem(my_z + oz, count_z)
                )
                from_x = lax.rem(my_x + count_x - ox, count_x)
                from_y = lax.rem(my_y + count_y - oy, count_y)
                from_z = lax.rem(my_z + count_z - oz, count_z)
                peers.append((step, towards, (from_x * count_y + from_y) * count_z + from_z))

            def for_peers(act, sending):
                for step, towards, source in peers:
                    act(reduce_copy(step, towards, me if sending else source))
        else:

            def for_peers(act, sending):
                def one(step, carry):
                    source = me if sending else lax.rem(me + devices - step, devices)
                    act(reduce_copy(step, coords(lax.rem(me + step, devices)), source))
                    return carry

                lax.fori_loop(1, devices, one, 0)

        for_peers(lambda copy: copy.start(), True)
        parts[me] = part[...]
        for_peers(lambda copy: copy.wait_recv(), False)
        found_parts = parts[...]
        count = devices
        while count > 1:
            half = count // 2
            rest = found_parts[2 * half :]
            found_parts = found_parts[:half] + found_parts[half : 2 * half]
            if count % 2:
                found_parts = jnp.concatenate([found_parts, rest], axis=0)
            count = count - half
        total_row = jnp.broadcast_to(found_parts[0], (rows, pair_pad))

        def entry(mine, other):
            slot = pair_slot[max(mine, other), min(mine, other)]
            return jnp.broadcast_to(total_row[:, slot : slot + 1], (rows, lanes))

        size = rhs * ITERS
        matrix = {}
        target = {}
        for i in range(size):
            for j in range(i + 1):
                matrix[i, j] = entry(rhs + i, rhs + j)
            for r in range(rhs):
                target[i, r] = entry(rhs + i, r)
        inverse = {}
        for k in range(size):
            inverse[k] = 1.0 / matrix[k, k]
            for i in range(k + 1, size):
                ratio = matrix[i, k] * inverse[k]
                for j in range(k + 1, i + 1):
                    matrix[i, j] = matrix[i, j] - ratio * matrix[j, k]
                for r in range(rhs):
                    target[i, r] = target[i, r] - ratio * target[k, r]
        weights = {}
        for k in range(size - 1, -1, -1):
            for r in range(rhs):
                accum = target[k, r]
                for later in range(k + 1, size):
                    accum = accum - matrix[later, k] * weights[later, r]
                weights[k, r] = accum * inverse[k]
        for r in range(rhs):
            for c in range(comp):
                found = jnp.zeros((rows, lanes), jnp.float32)
                left = right_ref[r * comp + c]
                for j in range(size):
                    found = found + weights[j, r] * values(j // rhs)[(j % rhs) * comp + c]
                    left = left - weights[j, r] * prods[j // rhs, (j % rhs) * comp + c]
                sol_ref[r * comp + c] = found
                res_ref[r * comp + c] = left

        for kind in range(KINDS):
            for plane in range(planes):

                def layer():
                    for turn in range(ITERS):
                        for group in range(groups):
                            if kind == 0:
                                whole = halo_rows.at[turn, group, plane, :, pl.ds(0, 2)]
                            elif kind < 3:
                                whole = halo_cols.at[turn, group, plane, kind - 1]
                            elif kind < 5:
                                whole = halo_corner.at[turn, group, plane, kind - 3, pl.ds(0, 2)]
                            elif plane > 0:
                                whole = far_plane.at[turn, group, plane - 1]
                            else:
                                continue
                            remote(whole, whole, kind, turn, group, beside(1, 0, 0)).wait_send()

                in_layer((0, 1, -1, 1, -1, 0)[kind], layer)
        for_peers(lambda copy: copy.wait_send(), True)

    copies = (ITERS, groups, planes)
    scratch = [
        pltpu.VMEM((fields,) + full, jnp.float32),
        pltpu.VMEM((ITERS - 1, fields) + full, jnp.float32),
        pltpu.VMEM((ITERS, fields) + full, jnp.float32),
        pltpu.VMEM((27, comp * comp) + full, jnp.bfloat16),
        pltpu.VMEM((planes, 9, comp * comp) + full, jnp.float32),
        pltpu.VMEM((ITERS, groups) + full, jnp.float32),
        pltpu.VMEM((ITERS, groups, planes - 1, span) + full, jnp.float32),
        pltpu.VMEM(copies + (span,) + full, jnp.float32),
        pltpu.VMEM(copies + (2,) + full, jnp.float32),
        pltpu.VMEM(copies + (2,) + full, jnp.float32),
        pltpu.VMEM((pair_pad, lanes), jnp.float32),
        pltpu.VMEM((1, pair_pad), jnp.float32),
        pltpu.VMEM((devices, 1, pair_pad), jnp.float32),
        pltpu.SemaphoreType.DMA,
        pltpu.SemaphoreType.DMA,
        pltpu.SemaphoreType.DMA((KINDS,)),
        pltpu.SemaphoreType.DMA((ITERS, groups, KINDS * planes)),
        pltpu.SemaphoreType.DMA((devices,)),
        pltpu.SemaphoreType.DMA((devices,)),
    ]
    return kernel, scratch


def hand_over(found_ref, left_ref, sol_ref, res_ref, sem):
    copies = [
        pltpu.make_async_copy(found_ref, sol_ref, sem.at[0]),
        pltpu.make_async_copy(left_ref, res_ref, sem.at[1]),
    ]
    for copy in copies:
        copy.start()
    for copy in copies:
        copy.wait()


def shards(sizes, right_side, jacobian):
    rhs, comp, extent_x, rows, lanes = right_side.shape
    assert extent_x == 1
    kernel, scratch = make_kernel(sizes, rhs, comp, rows, lanes)
    shape = (rhs * comp, rows, lanes)
    vmem = pl.BlockSpec(memory_space=pltpu.VMEM)
    hbm = pl.BlockSpec(memory_space=pltpu.HBM)
    found, left = pl.pallas_call(
        kernel,
        out_shape=(pltpu.VMEM(shape, jnp.float32),) * 2,
        in_specs=[hbm, hbm],
        out_specs=(vmem, vmem),
        scratch_shapes=scratch,
        compiler_params=pltpu.CompilerParams(collective_id=0, has_side_effects=True),
    )(
        right_side.reshape(shape),
        jacobian.reshape(27, comp * comp, rows, lanes),
    )
    found, left = pl.pallas_call(
        hand_over,
        out_shape=(jax.ShapeDtypeStruct(shape, jnp.float32),) * 2,
        in_specs=[vmem, vmem],
        out_specs=(hbm, hbm),
        scratch_shapes=[pltpu.SemaphoreType.DMA((2,))],
        compiler_params=pltpu.CompilerParams(vmem_limit_bytes=24 * 2**20),
    )(found, left)
    return found.reshape(right_side.shape), left.reshape(right_side.shape)


def solution(mesh):
    sizes = tuple(mesh.shape[axis] for axis in AXES)
    in_specs = (P(None, None, *AXES), P(None, None, None, *AXES))
    out_specs = (P(None, None, *AXES), P(None, None, *AXES))
    return jax.shard_map(
        functools.partial(shards, sizes), mesh=mesh, in_specs=in_specs, out_specs=out_specs, check_vma=False
    )
```

time: 28.3 us -> 27 us (0.954)
  Pallas kernels: 27.5 us -> 26.2 us
    pallas_call x1, Pallas kernels: 26.9 us -> 25.5 us  [shards(): pl.pallas_call(kernel, out_shape=(pltpu.VMEM(shape, jnp.float32),) * 2, i...]
where the time goes in v2:
time: 27 us; the launch traced here: 26.8 us
  Pallas kernels  26.2 us (97%)
  between operations  0.64 us (2%)
    pallas_call x1, Pallas kernels, shards(): pl.pallas_call(kernel, out_shape=(pltpu.VMEM(shape, jnp.float32),) * 2, i...  25.5 us
    pallas_call x1, Pallas kernels, shards(): pl.pallas_call(hand_over, out_shape=(jax.ShapeDtypeStruct(shape, jnp.floa...  0.68 us

profile of v2, /device:TPU:0, one launch (start us, length us, event | category | flops | bytes accessed | tf_op | source)
XLA Modules:
  0.0 26.8 jit_solution(11069822953514659799)
XLA Ops:
  0.6 25.5 %shard_map.41 = (f32[20,8,128]{2,1,0:T(8,128)S(1)}, f32[20,8,128]{2,1,0:T(8,128)S(1)}) custom-call(f32[20,8,128]{2,1,0:T(8,128)} %bitcast.9, bf16[27,25,8,128]{3,2,1,0:T(8,128)(2,1)} %bitcast.8), custom_call_target="tpu_custom_call" | custom-call | tf_op jit(solution)/shard_map/pallas_call | solution.py:428
  26.1 0.7 %shard_map.42 = (f32[20,8,128]{2,1,0:T(8,128)}, f32[20,8,128]{2,1,0:T(8,128)}) custom-call(f32[20,8,128]{2,1,0:T(8,128)S(1)} %get-tuple-element.6.found_ref, f32[20,8,128]{2,1,0:T(8,128)S(1)} %get-tuple-element.7.left_ref), custom_call_target="tpu_custom_call" | custom-call | tf_op jit(solution)/shard_map/pallas_call | solution.py:439

commit v3 on v2

--- a/solution.py
+++ b/solution.py
@@ -12,7 +12,7 @@
 SHIFT = 9.0
 MESH = pl.DeviceIdType.MESH
 AXES = ("gx", "gy", "gz")
-GROUPS = 4
+GROUPS = 2
 KINDS = 6
 
 
@@ -108,7 +108,7 @@
                 src_ref=source,
                 dst_ref=target,
                 send_sem=send_sem.at[kind % KINDS],
-                recv_sem=recv_sem.at[turn, group, kind],
+                recv_sem=recv_sem.at[turn % 2, group, kind],
                 device_id=device,
                 device_id_type=MESH,
             )
@@ -250,11 +250,15 @@
 
         for turn in range(ITERS):
             for group in range(groups):
-                totals = {}
-                for plane in range(planes):
+                wait_edges(turn, group, 0)
+                totals = stencil(turn, group, 0, {})
+                for at in range(span):
+                    prods[turn, group * span + at] = totals[at, 0] + totals[at, 1]
+            for group in range(groups):
+                totals = {(at, 0): prods[turn, group * span + at] for at in range(span)}
+                for plane in range(1, planes):
                     wait_edges(turn, group, plane)
-                    if plane > 0:
-                        wait_far(turn, group, plane)
+                    wait_far(turn, group, plane)
                     totals = stencil(turn, group, plane, totals)
                 found = [totals[at, 0] + totals[at, 1] for at in range(span)]
                 for at in range(span):
@@ -265,16 +269,20 @@
                         basis[turn, group * span + at] = found[at]
                     pack(turn + 1, group, found)
                     send(turn + 1, group)
-                for r in range(group * each, (group + 1) * each):
+                else:
+                    for r in range(group * each, (group + 1) * each):
+                        dots(rhs * (turn + 1) + r)
+            if turn < ITERS - 1:
+                for r in range(rhs):
                     dots(rhs * (turn + 1) + r)
 
         part[...] = jnp.sum(jnp.transpose(sums[...]), axis=0, keepdims=True)
-        def reduce_copy(step, towards, source):
+        def reduce_copy(towards, source, target):
             return pltpu.make_async_remote_copy(
-                src_ref=part,
-                dst_ref=parts.at[source],
-                send_sem=red_send.at[step],
-                recv_sem=red_recv.at[step],
+                src_ref=source,
+                dst_ref=target,
+                send_sem=red_send,
+                recv_sem=red_recv,
                 device_id=towards,
                 device_id_type=MESH,
             )
@@ -284,34 +292,43 @@
                 itertools.product(range(count_x), range(count_y), range(count_z)),
                 key=lambda at: (-min(at[1], count_y - at[1]), -at[0], at[2]),
             )
-            peers = []
-            for step, (ox, oy, oz) in enumerate(offsets):
-                if (ox, oy, oz) == (0, 0, 0):
-                    continue
-                towards = (
-                    lax.rem(my_x + ox, count_x), lax.rem(my_y + oy, count_y), lax.rem(my_z + oz, count_z)
-                )
-                from_x = lax.rem(my_x + count_x - ox, count_x)
-                from_y = lax.rem(my_y + count_y - oy, count_y)
-                from_z = lax.rem(my_z + count_z - oz, count_z)
-                peers.append((step, towards, (from_x * count_y + from_y) * count_z + from_z))
-
-            def for_peers(act, sending):
-                for step, towards, source in peers:
-                    act(reduce_copy(step, towards, me if sending else source))
+            for ox, oy, oz in offsets:
+                if (ox, oy, oz) != (0, 0, 0):
+                    towards = (
+                        lax.rem(my_x + ox, count_x), lax.rem(my_y + oy, count_y), lax.rem(my_z + oz, count_z)
+                    )
+                    reduce_copy(towards, part, parts.at[me]).start()
         else:
 
-            def for_peers(act, sending):
-                def one(step, carry):
-                    source = me if sending else lax.rem(me + devices - step, devices)
-                    act(reduce_copy(step, coords(lax.rem(me + step, devices)), source))
-                    return carry
-
-                lax.fori_loop(1, devices, one, 0)
-
-        for_peers(lambda copy: copy.start(), True)
+            def begin(step, carry):
+                reduce_copy(coords(lax.rem(me + step, devices)), part, parts.at[me]).start()
+                return carry
+
+            lax.fori_loop(1, devices, begin, 0)
         parts[me] = part[...]
-        for_peers(lambda copy: copy.wait_recv(), False)
+        for kind in range(KINDS):
+            for plane in range(planes):
+
+                def layer():
+                    for turn in range(ITERS):
+                        for group in range(groups):
+                            if kind == 0:
+                                whole = halo_rows.at[turn, group, plane, :, pl.ds(0, 2)]
+                            elif kind < 3:
+                                whole = halo_cols.at[turn, group, plane, kind - 1]
+                            elif kind < 5:
+                                whole = halo_corner.at[turn, group, plane, kind - 3, pl.ds(0, 2)]
+                            elif plane > 0:
+                                whole = far_plane.at[turn, group, plane - 1]
+                            else:
+                                continue
+                            remote(whole, whole, kind, turn, group, beside(1, 0, 0)).wait_send()
+
+                in_layer((0, 1, -1, 1, -1, 0)[kind], layer)
+        others = parts.at[pl.ds(0, devices - 1)]
+        all_others = reduce_copy(beside(1, 0, 0), others, others)
+        all_others.wait_recv()
+        all_others.wait_send()
         found_parts = parts[...]
         count = devices
         while count > 1:
@@ -347,40 +364,18 @@
         weights = {}
         for k in range(size - 1, -1, -1):
             for r in range(rhs):
-                accum = target[k, r]
-                for later in range(k + 1, size):
-                    accum = accum - matrix[later, k] * weights[later, r]
-                weights[k, r] = accum * inverse[k]
+                weights[k, r] = target[k, r] * inverse[k]
+                for prior in range(k):
+                    target[prior, r] = target[prior, r] - matrix[k, prior] * weights[k, r]
         for r in range(rhs):
             for c in range(comp):
                 found = jnp.zeros((rows, lanes), jnp.float32)
                 left = right_ref[r * comp + c]
-                for j in range(size):
+                for j in range(size - 1, -1, -1):
                     found = found + weights[j, r] * values(j // rhs)[(j % rhs) * comp + c]
                     left = left - weights[j, r] * prods[j // rhs, (j % rhs) * comp + c]
                 sol_ref[r * comp + c] = found
                 res_ref[r * comp + c] = left
-
-        for kind in range(KINDS):
-            for plane in range(planes):
-
-                def layer():
-                    for turn in range(ITERS):
-                        for group in range(groups):
-                            if kind == 0:
-                                whole = halo_rows.at[turn, group, plane, :, pl.ds(0, 2)]
-                            elif kind < 3:
-                                whole = halo_cols.at[turn, group, plane, kind - 1]
-                            elif kind < 5:
-                                whole = halo_corner.at[turn, group, plane, kind - 3, pl.ds(0, 2)]
-                            elif plane > 0:
-                                whole = far_plane.at[turn, group, plane - 1]
-                            else:
-                                continue
-                            remote(whole, whole, kind, turn, group, beside(1, 0, 0)).wait_send()
-
-                in_layer((0, 1, -1, 1, -1, 0)[kind], layer)
-        for_peers(lambda copy: copy.wait_send(), True)
 
     copies = (ITERS, groups, planes)
     scratch = [
@@ -400,9 +395,9 @@
         pltpu.SemaphoreType.DMA,
         pltpu.SemaphoreType.DMA,
         pltpu.SemaphoreType.DMA((KINDS,)),
-        pltpu.SemaphoreType.DMA((ITERS, groups, KINDS * planes)),
-        pltpu.SemaphoreType.DMA((devices,)),
-        pltpu.SemaphoreType.DMA((devices,)),
+        pltpu.SemaphoreType.DMA((2, groups, KINDS * planes)),
+        pltpu.SemaphoreType.DMA,
+        pltpu.SemaphoreType.DMA,
     ]
     return kernel, scratch
 

time: 27 us -> 25.9 us (0.959)
  Pallas kernels: 26.2 us -> 25.1 us
    pallas_call x1, Pallas kernels: 25.5 us -> 24.4 us  [shards(): pl.pallas_call(kernel, out_shape=(pltpu.VMEM(shape, jnp.float32),) * 2, i...]
where the time goes in v3:
time: 25.9 us; the launch traced here: 25.8 us
  Pallas kernels  25.1 us (97%)
  between operations  0.64 us (2%)
    pallas_call x1, Pallas kernels, shards(): pl.pallas_call(kernel, out_shape=(pltpu.VMEM(shape, jnp.float32),) * 2, i...  24.4 us
    pallas_call x1, Pallas kernels, shards(): pl.pallas_call(hand_over, out_shape=(jax.ShapeDtypeStruct(shape, jnp.floa...  0.68 us

profile of v3, /device:TPU:0, one launch (start us, length us, event | category | flops | bytes accessed | tf_op | source)
XLA Modules:
  0.0 25.8 jit_solution(12849421771152139840)
XLA Ops:
  0.6 24.4 %shard_map.41 = (f32[20,8,128]{2,1,0:T(8,128)S(1)}, f32[20,8,128]{2,1,0:T(8,128)S(1)}) custom-call(f32[20,8,128]{2,1,0:T(8,128)} %bitcast.9, bf16[27,25,8,128]{3,2,1,0:T(8,128)(2,1)} %bitcast.8), custom_call_target="tpu_custom_call" | custom-call | tf_op jit(solution)/shard_map/pallas_call | solution.py:423
  25.1 0.7 %shard_map.42 = (f32[20,8,128]{2,1,0:T(8,128)}, f32[20,8,128]{2,1,0:T(8,128)}) custom-call(f32[20,8,128]{2,1,0:T(8,128)S(1)} %get-tuple-element.6.found_ref, f32[20,8,128]{2,1,0:T(8,128)S(1)} %get-tuple-element.7.left_ref), custom_call_target="tpu_custom_call" | custom-call | tf_op jit(solution)/shard_map/pallas_call | solution.py:434

commit v4 on v3

--- a/solution.py
+++ b/solution.py
@@ -37,7 +37,7 @@
 
     def kernel(
         right_hbm, jac_hbm, sol_ref, res_ref,
-        right_ref, basis, prods, jac_low, jac, packs,
+        right_ref, basis, prods, partial, jac_low, jac, packs,
         far_plane, halo_rows, halo_cols, halo_corner, sums, part, parts,
         right_sem, jac_sem, send_sem, recv_sem, red_send, red_recv,
     ):
@@ -176,39 +176,47 @@
             return pltpu.roll(value, 1 if way < 0 else rows - 1, 0)
 
         def stencil(turn, group, plane, totals):
-            low = jnp.where(below, pltpu.roll(halo_cols[turn, group, plane, 0], 1, 1), 0.0)
-            high = jnp.where(above, pltpu.roll(halo_cols[turn, group, plane, 1], lanes - 1, 1), 0.0)
-            mixed = jnp.where(lane % 2 == 1, low, high)
-            low = jnp.where(below, pltpu.roll(halo_corner[turn, group, plane, 0], 1, 1), 0.0)
-            high = jnp.where(above, pltpu.roll(halo_corner[turn, group, plane, 1], lanes - 1, 1), 0.0)
-            outer = jnp.where(lane % 2 == 1, low, high)
+            even = lane % 2 == 0
+
+            def edges(halo):
+                low = jnp.where(below, halo[turn, group, plane, 0], 0.0)
+                high = jnp.where(above, halo[turn, group, plane, 1], 0.0)
+                return jnp.where(even, low, high)
+
+            inner, outer = edges(halo_cols), edges(halo_corner)
             side = {-1: sub == 0, 1: sub == rows - 1}
-            columns = {0: mixed}
-            for dy in (-1, 1):
-                columns[dy] = jnp.where(side[dy], outer, turned(mixed, dy))
-            for at in range(span):
-                source = at % comp
-                r = at // comp
-                if plane == 0:
-                    value = values(turn)[group * span + at]
-                else:
-                    value = far_plane[turn, group, plane - 1, at]
-                beyond = halo_rows[turn, group, plane, at]
+            columns = {dy: jnp.where(side[dy], outer, turned(inner, dy)) for dy in (-1, 1)}
+            columns[0] = inner
+            for source in range(comp):
                 for dy in (0, -1, 1):
-                    line = value if dy == 0 else jnp.where(side[dy], beyond, turned(value, dy))
-                    edge = pltpu.roll(columns[dy], lanes - 2 * at - 1, 1)
-                    along = (
-                        jnp.where(lane == 0, edge, pltpu.roll(line, 1, 1)),
-                        line,
-                        jnp.where(lane == lanes - 1, edge, pltpu.roll(line, lanes - 1, 1)),
-                    )
-                    for dz in range(3):
+                    along = {}
+                    for r in range(each):
+                        at = r * comp + source
+                        if plane == 0:
+                            value = values(turn)[group * span + at]
+                        else:
+                            value = far_plane[turn, group, plane - 1, at]
+                        if dy != 0:
+                            value = jnp.where(side[dy], halo_rows[turn, group, plane, at], turned(value, dy))
+                        edge = pltpu.roll(columns[dy], lanes - 2 * at - 1, 1)
+                        along[r, 1] = value
+                        along[r, 0] = jnp.where(lane == lanes - 1, edge, value)
+                        along[r, 2] = jnp.where(lane == 0, edge, value)
+                    for dz in (1, 0, 2):
                         near = (dy + 1) * 3 + dz
                         for a in range(comp):
-                            found = jac[plane, near, a * comp + source] * along[dz]
-                            key = (r * comp + a, (source + dz) % 2)
-                            totals[key] = totals[key] + found if key in totals else found
+                            block = jac[plane, near, a * comp + source]
+                            for r in range(each):
+                                found = block * along[r, dz]
+                                key = (r * comp + a, dz)
+                                totals[key] = totals[key] + found if key in totals else found
             return totals
+
+        def joined(totals):
+            return [
+                totals[at, 1] + (pltpu.roll(totals[at, 0], 1, 1) + pltpu.roll(totals[at, 2], lanes - 1, 1))
+                for at in range(span)
+            ]
 
         def vector(index, c):
             if index < rhs:
@@ -234,33 +242,39 @@
             send(0, group)
         loads.wait()
 
-        def widen(near, carry):
-            for entry in range(comp * comp):
-                jac[0, near, entry] = jac_low[9 + near, entry].astype(jnp.float32)
-                first = jac_low[near, entry].astype(jnp.float32)
-                last = jac_low[18 + near, entry].astype(jnp.float32)
-                if merged:
-                    jac[1, near, entry] = first + last
-                else:
-                    jac[1, near, entry] = first
-                    jac[2, near, entry] = last
+        def widen(line, carry):
+            for dz, shift in enumerate((lanes - 1, 0, 1)):
+                near = line * 3 + dz
+
+                def block(step_x, entry):
+                    found = jac_low[9 * step_x + near, entry].astype(jnp.float32)
+                    return pltpu.roll(found, shift, 1) if shift else found
+
+                for entry in range(comp * comp):
+                    jac[0, near, entry] = block(1, entry)
+                    if merged:
+                        found = jac_low[near, entry].astype(jnp.float32) + jac_low[18 + near, entry].astype(jnp.float32)
+                        jac[1, near, entry] = pltpu.roll(found, shift, 1) if shift else found
+                    else:
+                        jac[1, near, entry] = block(0, entry)
+                        jac[2, near, entry] = block(2, entry)
             return carry
 
-        lax.fori_loop(0, 9, widen, 0)
+        lax.fori_loop(0, 3, widen, 0)
 
         for turn in range(ITERS):
             for group in range(groups):
                 wait_edges(turn, group, 0)
                 totals = stencil(turn, group, 0, {})
-                for at in range(span):
-                    prods[turn, group * span + at] = totals[at, 0] + totals[at, 1]
+                for (at, dz), total in totals.items():
+                    partial[group, dz, at] = total
             for group in range(groups):
-                totals = {(at, 0): prods[turn, group * span + at] for at in range(span)}
+                totals = {(at, dz): partial[group, dz, at] for at in range(span) for dz in range(3)}
                 for plane in range(1, planes):
                     wait_edges(turn, group, plane)
                     wait_far(turn, group, plane)
                     totals = stencil(turn, group, plane, totals)
-                found = [totals[at, 0] + totals[at, 1] for at in range(span)]
+                found = joined(totals)
                 for at in range(span):
                     prods[turn, group * span + at] = found[at]
                 if turn < ITERS - 1:
@@ -367,21 +381,26 @@
                 weights[k, r] = target[k, r] * inverse[k]
                 for prior in range(k):
                     target[prior, r] = target[prior, r] - matrix[k, prior] * weights[k, r]
-        for r in range(rhs):
-            for c in range(comp):
-                found = jnp.zeros((rows, lanes), jnp.float32)
-                left = right_ref[r * comp + c]
-                for j in range(size - 1, -1, -1):
-                    found = found + weights[j, r] * values(j // rhs)[(j % rhs) * comp + c]
-                    left = left - weights[j, r] * prods[j // rhs, (j % rhs) * comp + c]
-                sol_ref[r * comp + c] = found
-                res_ref[r * comp + c] = left
+        for c in range(comp):
+            found = {}
+            left = {r: right_ref[r * comp + c] for r in range(rhs)}
+            for j in range(size - 1, -1, -1):
+                direction = values(j // rhs)[(j % rhs) * comp + c]
+                product = prods[j // rhs, (j % rhs) * comp + c]
+                for r in range(rhs):
+                    term = weights[j, r] * direction
+                    found[r] = found[r] + term if r in found else term
+                    left[r] = left[r] - weights[j, r] * product
+            for r in range(rhs):
+                sol_ref[r * comp + c] = found[r]
+                res_ref[r * comp + c] = left[r]
 
     copies = (ITERS, groups, planes)
     scratch = [
         pltpu.VMEM((fields,) + full, jnp.float32),
         pltpu.VMEM((ITERS - 1, fields) + full, jnp.float32),
         pltpu.VMEM((ITERS, fields) + full, jnp.float32),
+        pltpu.VMEM((groups, 3, span) + full, jnp.float32),
         pltpu.VMEM((27, comp * comp) + full, jnp.bfloat16),
         pltpu.VMEM((planes, 9, comp * comp) + full, jnp.float32),
         pltpu.VMEM((ITERS, groups) + full, jnp.float32),

time: 25.9 us -> 25.8 us (level)
  no operation moved by 1% of the time
where the time goes in v4:
time: 25.8 us; the launch traced here: 25.6 us
  Pallas kernels  25 us (97%)
  between operations  0.64 us (2%)
    pallas_call x1, Pallas kernels, shards(): pl.pallas_call(kernel, out_shape=(pltpu.VMEM(shape, jnp.float32),) * 2, i...  24.3 us
    pallas_call x1, Pallas kernels, shards(): pl.pallas_call(hand_over, out_shape=(jax.ShapeDtypeStruct(shape, jnp.floa...  0.68 us

profile of v4, /device:TPU:0, one launch (start us, length us, event | category | flops | bytes accessed | tf_op | source)
XLA Modules:
  0.0 25.6 jit_solution(17274373917749092402)
XLA Ops:
  0.6 24.3 %shard_map.41 = (f32[20,8,128]{2,1,0:T(8,128)S(1)}, f32[20,8,128]{2,1,0:T(8,128)S(1)}) custom-call(f32[20,8,128]{2,1,0:T(8,128)} %bitcast.9, bf16[27,25,8,128]{3,2,1,0:T(8,128)(2,1)} %bitcast.8), custom_call_target="tpu_custom_call" | custom-call | tf_op jit(solution)/shard_map/pallas_call | solution.py:442
  24.9 0.7 %shard_map.42 = (f32[20,8,128]{2,1,0:T(8,128)}, f32[20,8,128]{2,1,0:T(8,128)}) custom-call(f32[20,8,128]{2,1,0:T(8,128)S(1)} %get-tuple-element.6.found_ref, f32[20,8,128]{2,1,0:T(8,128)S(1)} %get-tuple-element.7.left_ref), custom_call_target="tpu_custom_call" | custom-call | tf_op jit(solution)/shard_map/pallas_call | solution.py:453

commit v5 on v4

--- a/solution.py
+++ b/solution.py
@@ -13,7 +13,7 @@
 MESH = pl.DeviceIdType.MESH
 AXES = ("gx", "gy", "gz")
 GROUPS = 2
-KINDS = 6
+KINDS = 5
 
 
 def make_kernel(sizes, rhs, comp, rows, lanes):
@@ -97,30 +97,27 @@
         def values(turn):
             return right_ref if turn == 0 else basis.at[turn - 1]
 
-        def pack(turn, group, found):
-            packed = jnp.zeros(full, jnp.float32)
-            for at in range(span):
-                packed = jnp.where(lane // 2 == at, pltpu.roll(found[at], 2 * at + 1, 1), packed)
-            packs[turn, group] = packed
-
-        def remote(source, target, kind, turn, group, device):
+        def packed_with(packed, first, found):
+            for at, value in enumerate(found, first):
+                packed = jnp.where(lane // 2 == at, pltpu.roll(value, 2 * at + 1, 1), packed)
+            return packed
+
+        def remote(source, target, kind, turn, plane, device):
             return pltpu.make_async_remote_copy(
                 src_ref=source,
                 dst_ref=target,
-                send_sem=send_sem.at[kind % KINDS],
-                recv_sem=recv_sem.at[turn % 2, group, kind],
+                send_sem=send_sem.at[min(kind, KINDS)],
+                recv_sem=recv_sem.at[turn % 2, plane, kind],
                 device_id=device,
                 device_id_type=MESH,
             )
 
-        def send(turn, group):
-            mine = pl.ds(group * span, span)
+        def send_edges(turn):
             for dz in (1, -1, 0):
                 side_z = 0 if dz == 1 else 1
 
                 def layer():
                     for plane in reversed(range(planes)):
-                        kind = KINDS * plane
                         for dy in (1, -1, 0):
                             device = beside(plane_steps[plane], dy, dz)
                             edge = pl.ds(rows - 1 if dy == 1 else 0, 1)
@@ -128,76 +125,68 @@
                             if dy == 0 and dz == 0:
                                 continue
                             if dz == 0:
-                                copy = remote(
-                                    values(turn).at[mine, edge], halo_rows.at[turn, group, plane, :, place],
-                                    kind, turn, group, device,
-                                )
+                                source, target, kind = values(turn).at[:, edge], halo_rows.at[turn, plane, :, place], 0
                             elif dy == 0:
-                                copy = remote(
-                                    packs.at[turn, group], halo_cols.at[turn, group, plane, side_z],
-                                    kind + 1 + side_z, turn, group, device,
-                                )
+                                source, target, kind = packs.at[turn], halo_cols.at[turn, plane, side_z], 1 + side_z
                             else:
-                                copy = remote(
-                                    packs.at[turn, group, edge], halo_corner.at[turn, group, plane, side_z, place],
-                                    kind + 3 + side_z, turn, group, device,
-                                )
-                            copy.start()
+                                source, target = packs.at[turn, edge], halo_corner.at[turn, plane, side_z, place]
+                                kind = 3 + side_z
+                            remote(source, target, kind, turn, plane, device).start()
 
                 in_layer(dz, layer)
+
+        def send_far(turn, group):
             for plane in range(1, planes):
                 remote(
-                    values(turn).at[mine], far_plane.at[turn, group, plane - 1],
-                    KINDS * plane + 5, turn, group, beside(plane_steps[plane], 0, 0),
+                    values(turn).at[pl.ds(group * span, span)], far_plane.at[turn, plane - 1, pl.ds(group * span, span)],
+                    KINDS + group, turn, plane, beside(plane_steps[plane], 0, 0),
                 ).start()
 
-        def wait_edges(turn, group, plane):
-            kind = KINDS * plane
+        def wait_edges(turn, plane):
             here = beside(1, 0, 0)
-            both = halo_rows.at[turn, group, plane, :, pl.ds(0, 2)]
-            remote(both, both, kind, turn, group, here).wait_recv()
+            both = halo_rows.at[turn, plane, :, pl.ds(0, 2)]
+            remote(both, both, 0, turn, plane, here).wait_recv()
             for side_z, dz in ((0, -1), (1, 1)):
 
                 def layer():
-                    column = halo_cols.at[turn, group, plane, side_z]
-                    remote(column, column, kind + 1 + side_z, turn, group, here).wait_recv()
-                    corner = halo_corner.at[turn, group, plane, side_z, pl.ds(0, 2)]
-                    remote(corner, corner, kind + 3 + side_z, turn, group, here).wait_recv()
+                    column = halo_cols.at[turn, plane, side_z]
+                    remote(column, column, 1 + side_z, turn, plane, here).wait_recv()
+                    corner = halo_corner.at[turn, plane, side_z, pl.ds(0, 2)]
+                    remote(corner, corner, 3 + side_z, turn, plane, here).wait_recv()
 
                 in_layer(dz, layer)
 
         def wait_far(turn, group, plane):
-            whole = far_plane.at[turn, group, plane - 1]
-            remote(whole, whole, KINDS * plane + 5, turn, group, beside(1, 0, 0)).wait_recv()
+            whole = far_plane.at[turn, plane - 1, pl.ds(group * span, span)]
+            remote(whole, whole, KINDS + group, turn, plane, beside(1, 0, 0)).wait_recv()
 
         def turned(value, way):
             if way == 0:
                 return value
             return pltpu.roll(value, 1 if way < 0 else rows - 1, 0)
 
-        def stencil(turn, group, plane, totals):
-            even = lane % 2 == 0
-
+        side = {-1: sub == 0, 1: sub == rows - 1}
+
+        def edge_columns(turn, plane):
             def edges(halo):
-                low = jnp.where(below, halo[turn, group, plane, 0], 0.0)
-                high = jnp.where(above, halo[turn, group, plane, 1], 0.0)
-                return jnp.where(even, low, high)
+                low = jnp.where(below, halo[turn, plane, 0], 0.0)
+                high = jnp.where(above, halo[turn, plane, 1], 0.0)
+                return jnp.where(lane % 2 == 0, low, high)
 
             inner, outer = edges(halo_cols), edges(halo_corner)
-            side = {-1: sub == 0, 1: sub == rows - 1}
             columns = {dy: jnp.where(side[dy], outer, turned(inner, dy)) for dy in (-1, 1)}
             columns[0] = inner
+            return columns
+
+        def stencil(turn, group, plane, columns, totals):
             for source in range(comp):
                 for dy in (0, -1, 1):
                     along = {}
                     for r in range(each):
-                        at = r * comp + source
-                        if plane == 0:
-                            value = values(turn)[group * span + at]
-                        else:
-                            value = far_plane[turn, group, plane - 1, at]
+                        at = group * span + r * comp + source
+                        value = values(turn)[at] if plane == 0 else far_plane[turn, plane - 1, at]
                         if dy != 0:
-                            value = jnp.where(side[dy], halo_rows[turn, group, plane, at], turned(value, dy))
+                            value = jnp.where(side[dy], halo_rows[turn, plane, at], turned(value, dy))
                         edge = pltpu.roll(columns[dy], lanes - 2 * at - 1, 1)
                         along[r, 1] = value
                         along[r, 0] = jnp.where(lane == lanes - 1, edge, value)
@@ -235,11 +224,11 @@
         for slot in range(len(pair_list), pair_pad):
             sums[slot : slot + 1, :] = jnp.zeros((1, lanes), jnp.float32)
         right_load.wait()
+        packs[0] = packed_with(jnp.zeros(full, jnp.float32), 0, [right_ref[at] for at in range(fields)])
+        pl.semaphore_wait(barrier, greeted)
+        send_edges(0)
         for group in range(groups):
-            pack(0, group, [right_ref[group * span + at] for at in range(span)])
-        pl.semaphore_wait(barrier, greeted)
-        for group in range(groups):
-            send(0, group)
+            send_far(0, group)
         loads.wait()
 
         def widen(line, carry):
@@ -263,26 +252,34 @@
         lax.fori_loop(0, 3, widen, 0)
 
         for turn in range(ITERS):
+            wait_edges(turn, 0)
+            columns = edge_columns(turn, 0)
             for group in range(groups):
-                wait_edges(turn, group, 0)
-                totals = stencil(turn, group, 0, {})
-                for (at, dz), total in totals.items():
+                for (at, dz), total in stencil(turn, group, 0, columns, {}).items():
                     partial[group, dz, at] = total
+            columns = {}
+            packed = jnp.zeros(full, jnp.float32)
             for group in range(groups):
+                first = group * span
                 totals = {(at, dz): partial[group, dz, at] for at in range(span) for dz in range(3)}
                 for plane in range(1, planes):
-                    wait_edges(turn, group, plane)
+                    if group == 0:
+                        wait_edges(turn, plane)
+                        columns[plane] = edge_columns(turn, plane)
                     wait_far(turn, group, plane)
-                    totals = stencil(turn, group, plane, totals)
+                    totals = stencil(turn, group, plane, columns[plane], totals)
                 found = joined(totals)
                 for at in range(span):
-                    prods[turn, group * span + at] = found[at]
+                    prods[turn, first + at] = found[at]
                 if turn < ITERS - 1:
-                    found = [found[at] - SHIFT * values(turn)[group * span + at] for at in range(span)]
+                    found = [found[at] - SHIFT * values(turn)[first + at] for at in range(span)]
                     for at in range(span):
-                        basis[turn, group * span + at] = found[at]
-                    pack(turn + 1, group, found)
-                    send(turn + 1, group)
+                        basis[turn, first + at] = found[at]
+                    packed = packed_with(packed, first, found)
+                    if group == groups - 1:
+                        packs[turn + 1] = packed
+                        send_edges(turn + 1)
+                    send_far(turn + 1, group)
                 else:
                     for r in range(group * each, (group + 1) * each):
                         dots(rhs * (turn + 1) + r)
@@ -320,23 +317,22 @@
 
             lax.fori_loop(1, devices, begin, 0)
         parts[me] = part[...]
-        for kind in range(KINDS):
+        for kind in range(KINDS + 1):
             for plane in range(planes):
 
                 def layer():
                     for turn in range(ITERS):
-                        for group in range(groups):
-                            if kind == 0:
-                                whole = halo_rows.at[turn, group, plane, :, pl.ds(0, 2)]
-                            elif kind < 3:
-                                whole = halo_cols.at[turn, group, plane, kind - 1]
-                            elif kind < 5:
-                                whole = halo_corner.at[turn, group, plane, kind - 3, pl.ds(0, 2)]
-                            elif plane > 0:
-                                whole = far_plane.at[turn, group, plane - 1]
-                            else:
-                                continue
-                            remote(whole, whole, kind, turn, group, beside(1, 0, 0)).wait_send()
+                        if kind == 0:
+                            whole = halo_rows.at[turn, plane, :, pl.ds(0, 2)]
+                        elif kind < 3:
+                            whole = halo_cols.at[turn, plane, kind - 1]
+                        elif kind < 5:
+                            whole = halo_corner.at[turn, plane, kind - 3, pl.ds(0, 2)]
+                        elif plane > 0:
+                            whole = far_plane.at[turn, plane - 1]
+                        else:
+                            continue
+                        remote(whole, whole, kind, turn, plane, beside(1, 0, 0)).wait_send()
 
                 in_layer((0, 1, -1, 1, -1, 0)[kind], layer)
         others = parts.at[pl.ds(0, devices - 1)]
@@ -395,7 +391,7 @@
                 sol_ref[r * comp + c] = found[r]
                 res_ref[r * comp + c] = left[r]
 
-    copies = (ITERS, groups, planes)
+    copies = (ITERS, planes)
     scratch = [
         pltpu.VMEM((fields,) + full, jnp.float32),
         pltpu.VMEM((ITERS - 1, fields) + full, jnp.float32),
@@ -403,9 +399,9 @@
         pltpu.VMEM((groups, 3, span) + full, jnp.float32),
         pltpu.VMEM((27, comp * comp) + full, jnp.bfloat16),
         pltpu.VMEM((planes, 9, comp * comp) + full, jnp.float32),
-        pltpu.VMEM((ITERS, groups) + full, jnp.float32),
-        pltpu.VMEM((ITERS, groups, planes - 1, span) + full, jnp.float32),
-        pltpu.VMEM(copies + (span,) + full, jnp.float32),
+        pltpu.VMEM((ITERS,) + full, jnp.float32),
+        pltpu.VMEM((ITERS, planes - 1, fields) + full, jnp.float32),
+        pltpu.VMEM(copies + (fields,) + full, jnp.float32),
         pltpu.VMEM(copies + (2,) + full, jnp.float32),
         pltpu.VMEM(copies + (2,) + full, jnp.float32),
         pltpu.VMEM((pair_pad, lanes), jnp.float32),
@@ -413,8 +409,8 @@
         pltpu.VMEM((devices, 1, pair_pad), jnp.float32),
         pltpu.SemaphoreType.DMA,
         pltpu.SemaphoreType.DMA,
-        pltpu.SemaphoreType.DMA((KINDS,)),
-        pltpu.SemaphoreType.DMA((2, groups, KINDS * planes)),
+        pltpu.SemaphoreType.DMA((KINDS + 1,)),
+        pltpu.SemaphoreType.DMA((2, planes, KINDS + groups)),
         pltpu.SemaphoreType.DMA,
         pltpu.SemaphoreType.DMA,
     ]

time: 25.8 us -> 25.5 us (0.988)
  Pallas kernels: 25 us -> 24.7 us
    pallas_call x1, Pallas kernels: 24.3 us -> 24 us  [shards(): pl.pallas_call(kernel, out_shape=(pltpu.VMEM(shape, jnp.float32),) * 2, i...]
where the time goes in v5:
time: 25.5 us; the launch traced here: 25.3 us
  Pallas kernels  24.7 us (97%)
  between operations  0.64 us (3%)
    pallas_call x1, Pallas kernels, shards(): pl.pallas_call(kernel, out_shape=(pltpu.VMEM(shape, jnp.float32),) * 2, i...  24 us
    pallas_call x1, Pallas kernels, shards(): pl.pallas_call(hand_over, out_shape=(jax.ShapeDtypeStruct(shape, jnp.floa...  0.68 us

profile of v5, /device:TPU:0, one launch (start us, length us, event | category | flops | bytes accessed | tf_op | source)
XLA Modules:
  0.0 25.3 jit_solution(14270694212751958358)
XLA Ops:
  0.6 24.0 %shard_map.41 = (f32[20,8,128]{2,1,0:T(8,128)S(1)}, f32[20,8,128]{2,1,0:T(8,128)S(1)}) custom-call(f32[20,8,128]{2,1,0:T(8,128)} %bitcast.9, bf16[27,25,8,128]{3,2,1,0:T(8,128)(2,1)} %bitcast.8), custom_call_target="tpu_custom_call" | custom-call | tf_op jit(solution)/shard_map/pallas_call | solution.py:438
  24.6 0.7 %shard_map.42 = (f32[20,8,128]{2,1,0:T(8,128)}, f32[20,8,128]{2,1,0:T(8,128)}) custom-call(f32[20,8,128]{2,1,0:T(8,128)S(1)} %get-tuple-element.6.found_ref, f32[20,8,128]{2,1,0:T(8,128)S(1)} %get-tuple-element.7.left_ref), custom_call_target="tpu_custom_call" | custom-call | tf_op jit(solution)/shard_map/pallas_call | solution.py:449

commit v6 on v5

--- a/solution.py
+++ b/solution.py
@@ -12,8 +12,17 @@
 SHIFT = 9.0
 MESH = pl.DeviceIdType.MESH
 AXES = ("gx", "gy", "gz")
-GROUPS = 2
+PAIRS = (2, 2)
+PIECES = (2, 1, 1)
+EARLY = 2
 KINDS = 5
+
+
+def parted(sizes, total):
+    if sum(sizes) != total:
+        sizes = (1,) * total
+    ends = list(itertools.accumulate(sizes))
+    return [range(end - size, end) for end, size in zip(ends, sizes)]
 
 
 def make_kernel(sizes, rhs, comp, rows, lanes):
@@ -24,9 +33,8 @@
     near_only = max(count_x // 2, count_y // 2, count_z - 1) <= ITERS
     plane_steps = (0, 1) if merged else (0, 1, -1)
     planes = len(plane_steps)
-    groups = GROUPS if rhs % GROUPS == 0 else rhs
-    each = rhs // groups
-    span = each * comp
+    near = parted(PAIRS, rhs)
+    away = parted(PIECES, rhs)
     pair_list = []
     for mine in range(rhs, rhs * (ITERS + 1)):
         for other in range(0, mine + 1):
@@ -135,11 +143,14 @@
 
                 in_layer(dz, layer)
 
-        def send_far(turn, group):
+        def piece(index):
+            return pl.ds(away[index].start * comp, len(away[index]) * comp)
+
+        def send_far(turn, index):
             for plane in range(1, planes):
                 remote(
-                    values(turn).at[pl.ds(group * span, span)], far_plane.at[turn, plane - 1, pl.ds(group * span, span)],
-                    KINDS + group, turn, plane, beside(plane_steps[plane], 0, 0),
+                    values(turn).at[piece(index)], far_plane.at[turn, plane - 1, piece(index)],
+                    KINDS + index, turn, plane, beside(plane_steps[plane], 0, 0),
                 ).start()
 
         def wait_edges(turn, plane):
@@ -156,9 +167,9 @@
 
                 in_layer(dz, layer)
 
-        def wait_far(turn, group, plane):
-            whole = far_plane.at[turn, plane - 1, pl.ds(group * span, span)]
-            remote(whole, whole, KINDS + group, turn, plane, beside(1, 0, 0)).wait_recv()
+        def wait_far(turn, index, plane):
+            whole = far_plane.at[turn, plane - 1, piece(index)]
+            remote(whole, whole, KINDS + index, turn, plane, beside(1, 0, 0)).wait_recv()
 
         def turned(value, way):
             if way == 0:
@@ -178,12 +189,12 @@
             columns[0] = inner
             return columns
 
-        def stencil(turn, group, plane, columns, totals):
+        def stencil(turn, chosen, plane, columns, totals):
             for source in range(comp):
                 for dy in (0, -1, 1):
                     along = {}
-                    for r in range(each):
-                        at = group * span + r * comp + source
+                    for r in chosen:
+                        at = r * comp + source
                         value = values(turn)[at] if plane == 0 else far_plane[turn, plane - 1, at]
                         if dy != 0:
                             value = jnp.where(side[dy], halo_rows[turn, plane, at], turned(value, dy))
@@ -192,20 +203,17 @@
                         along[r, 0] = jnp.where(lane == lanes - 1, edge, value)
                         along[r, 2] = jnp.where(lane == 0, edge, value)
                     for dz in (1, 0, 2):
-                        near = (dy + 1) * 3 + dz
+                        spot = (dy + 1) * 3 + dz
                         for a in range(comp):
-                            block = jac[plane, near, a * comp + source]
-                            for r in range(each):
+                            block = jac[plane, spot, a * comp + source]
+                            for r in chosen:
                                 found = block * along[r, dz]
                                 key = (r * comp + a, dz)
                                 totals[key] = totals[key] + found if key in totals else found
             return totals
 
-        def joined(totals):
-            return [
-                totals[at, 1] + (pltpu.roll(totals[at, 0], 1, 1) + pltpu.roll(totals[at, 2], lanes - 1, 1))
-                for at in range(span)
-            ]
+        def joined(totals, at):
+            return totals[at, 1] + (pltpu.roll(totals[at, 0], 1, 1) + pltpu.roll(totals[at, 2], lanes - 1, 1))
 
         def vector(index, c):
             if index < rhs:
@@ -227,8 +235,8 @@
         packs[0] = packed_with(jnp.zeros(full, jnp.float32), 0, [right_ref[at] for at in range(fields)])
         pl.semaphore_wait(barrier, greeted)
         send_edges(0)
-        for group in range(groups):
-            send_far(0, group)
+        for index in range(len(away)):
+            send_far(0, index)
         loads.wait()
 
         def widen(line, carry):
@@ -254,35 +262,38 @@
         for turn in range(ITERS):
             wait_edges(turn, 0)
             columns = edge_columns(turn, 0)
-            for group in range(groups):
-                for (at, dz), total in stencil(turn, group, 0, columns, {}).items():
-                    partial[group, dz, at] = total
+            for chosen in near:
+                for (at, dz), total in stencil(turn, chosen, 0, columns, {}).items():
+                    partial[dz, at] = total
             columns = {}
             packed = jnp.zeros(full, jnp.float32)
-            for group in range(groups):
-                first = group * span
-                totals = {(at, dz): partial[group, dz, at] for at in range(span) for dz in range(3)}
+            for index, chosen in enumerate(away):
+                span = range(chosen.start * comp, chosen.stop * comp)
+                totals = {(at, dz): partial[dz, at] for at in span for dz in range(3)}
                 for plane in range(1, planes):
-                    if group == 0:
+                    if index == 0:
                         wait_edges(turn, plane)
                         columns[plane] = edge_columns(turn, plane)
-                    wait_far(turn, group, plane)
-                    totals = stencil(turn, group, plane, columns[plane], totals)
-                found = joined(totals)
-                for at in range(span):
-                    prods[turn, first + at] = found[at]
-                if turn < ITERS - 1:
-                    found = [found[at] - SHIFT * values(turn)[first + at] for at in range(span)]
-                    for at in range(span):
-                        basis[turn, first + at] = found[at]
-                    packed = packed_with(packed, first, found)
-                    if group == groups - 1:
-                        packs[turn + 1] = packed
-                        send_edges(turn + 1)
-                    send_far(turn + 1, group)
-                else:
-                    for r in range(group * each, (group + 1) * each):
+                    wait_far(turn, index, plane)
+                    totals = stencil(turn, chosen, plane, columns[plane], totals)
+                found = [joined(totals, at) for at in span]
+                for at, value in zip(span, found):
+                    prods[turn, at] = value
+                if turn == ITERS - 1:
+                    for r in chosen:
                         dots(rhs * (turn + 1) + r)
+                    continue
+                found = [value - SHIFT * values(turn)[at] for at, value in zip(span, found)]
+                for at, value in zip(span, found):
+                    basis[turn, at] = value
+                packed = packed_with(packed, span.start, found)
+                if index < EARLY:
+                    send_far(turn + 1, index)
+                if index == len(away) - 1:
+                    packs[turn + 1] = packed
+                    send_edges(turn + 1)
+                    for later in range(EARLY, len(away)):
+                        send_far(turn + 1, later)
             if turn < ITERS - 1:
                 for r in range(rhs):
                     dots(rhs * (turn + 1) + r)
@@ -396,7 +407,7 @@
         pltpu.VMEM((fields,) + full, jnp.float32),
         pltpu.VMEM((ITERS - 1, fields) + full, jnp.float32),
         pltpu.VMEM((ITERS, fields) + full, jnp.float32),
-        pltpu.VMEM((groups, 3, span) + full, jnp.float32),
+        pltpu.VMEM((3, fields) + full, jnp.float32),
         pltpu.VMEM((27, comp * comp) + full, jnp.bfloat16),
         pltpu.VMEM((planes, 9, comp * comp) + full, jnp.float32),
         pltpu.VMEM((ITERS,) + full, jnp.float32),
@@ -410,7 +421,7 @@
         pltpu.SemaphoreType.DMA,
         pltpu.SemaphoreType.DMA,
         pltpu.SemaphoreType.DMA((KINDS + 1,)),
-        pltpu.SemaphoreType.DMA((2, planes, KINDS + groups)),
+        pltpu.SemaphoreType.DMA((2, planes, KINDS + len(away))),
         pltpu.SemaphoreType.DMA,
         pltpu.SemaphoreType.DMA,
     ]

time: 25.5 us -> 25.4 us (level)
  no operation moved by 1% of the time
where the time goes in v6:
time: 25.4 us; the launch traced here: 25.2 us
  Pallas kernels  24.6 us (97%)
  between operations  0.64 us (3%)
    pallas_call x1, Pallas kernels, shards(): pl.pallas_call(kernel, out_shape=(pltpu.VMEM(shape, jnp.float32),) * 2, i...  23.9 us
    pallas_call x1, Pallas kernels, shards(): pl.pallas_call(hand_over, out_shape=(jax.ShapeDtypeStruct(shape, jnp.floa...  0.68 us

profile of v6, /device:TPU:0, one launch (start us, length us, event | category | flops | bytes accessed | tf_op | source)
XLA Modules:
  0.0 25.2 jit_solution(3422528422560026478)
XLA Ops:
  0.6 23.9 %shard_map.41 = (f32[20,8,128]{2,1,0:T(8,128)S(1)}, f32[20,8,128]{2,1,0:T(8,128)S(1)}) custom-call(f32[20,8,128]{2,1,0:T(8,128)} %bitcast.9, bf16[27,25,8,128]{3,2,1,0:T(8,128)(2,1)} %bitcast.8), custom_call_target="tpu_custom_call" | custom-call | tf_op jit(solution)/shard_map/pallas_call | solution.py:449
  24.6 0.7 %shard_map.42 = (f32[20,8,128]{2,1,0:T(8,128)}, f32[20,8,128]{2,1,0:T(8,128)}) custom-call(f32[20,8,128]{2,1,0:T(8,128)S(1)} %get-tuple-element.6.found_ref, f32[20,8,128]{2,1,0:T(8,128)S(1)} %get-tuple-element.7.left_ref), custom_call_target="tpu_custom_call" | custom-call | tf_op jit(solution)/shard_map/pallas_call | solution.py:460

commit v7 on v6

--- a/solution.py
+++ b/solution.py
@@ -14,7 +14,7 @@
 AXES = ("gx", "gy", "gz")
 PAIRS = (2, 2)
 PIECES = (2, 1, 1)
-EARLY = 2
+EARLY = 1
 KINDS = 5
 
 

time: 25.4 us -> 25.4 us (level)
  no operation moved by 1% of the time
where the time goes in v7:
time: 25.4 us; the launch traced here: 25.2 us
  Pallas kernels  24.6 us (97%)
  between operations  0.64 us (3%)
    pallas_call x1, Pallas kernels, shards(): pl.pallas_call(kernel, out_shape=(pltpu.VMEM(shape, jnp.float32),) * 2, i...  23.9 us
    pallas_call x1, Pallas kernels, shards(): pl.pallas_call(hand_over, out_shape=(jax.ShapeDtypeStruct(shape, jnp.floa...  0.68 us

profile of v7, /device:TPU:0, one launch (start us, length us, event | category | flops | bytes accessed | tf_op | source)
XLA Modules:
  0.0 25.2 jit_solution(12644851067217802586)
XLA Ops:
  0.6 23.9 %shard_map.41 = (f32[20,8,128]{2,1,0:T(8,128)S(1)}, f32[20,8,128]{2,1,0:T(8,128)S(1)}) custom-call(f32[20,8,128]{2,1,0:T(8,128)} %bitcast.9, bf16[27,25,8,128]{3,2,1,0:T(8,128)(2,1)} %bitcast.8), custom_call_target="tpu_custom_call" | custom-call | tf_op jit(solution)/shard_map/pallas_call | solution.py:449
  24.6 0.7 %shard_map.42 = (f32[20,8,128]{2,1,0:T(8,128)}, f32[20,8,128]{2,1,0:T(8,128)}) custom-call(f32[20,8,128]{2,1,0:T(8,128)S(1)} %get-tuple-element.6.found_ref, f32[20,8,128]{2,1,0:T(8,128)S(1)} %get-tuple-element.7.left_ref), custom_call_target="tpu_custom_call" | custom-call | tf_op jit(solution)/shard_map/pallas_call | solution.py:460
